TPU v7x, 32 devices: a whole 2x2x4 slice. The times are simulated.
32 devices in a mesh: rep: 2 (over x), dp: 16 (over y, z, core).
Axes of the slice: x: 2, y: 2, z: 4, core: 2. Of those that a mesh axis runs over, the one named last changes fastest.
Arguments:
- x: bfloat16 [32, 2048, 1024], P(('rep', 'dp')), parts along dimension 0
- dy: bfloat16 [32, 2048, 1024], P(('rep', 'dp')), parts along dimension 0
- w_gate: bfloat16 [2, 1024, 4096], replicated
- w_up: bfloat16 [2, 1024, 4096], replicated
- w_down: bfloat16 [2, 4096, 1024], replicated
- m_w_gate: float32 [2, 1024, 4096], replicated
- m_w_up: float32 [2, 1024, 4096], replicated
- m_w_down: float32 [2, 4096, 1024], replicated
- v_w_gate: float32 [2, 1024, 4096], replicated
- v_w_up: float32 [2, 1024, 4096], replicated
- v_w_down: float32 [2, 4096, 1024], replicated
Outputs:
- output 1: bfloat16 [4, 1024, 4096], P('rep'), parts along dimension 0
- output 2: bfloat16 [4, 1024, 4096], P('rep'), parts along dimension 0
- output 3: bfloat16 [4, 4096, 1024], P('rep'), parts along dimension 0
- output 4: float32 [4, 1024, 4096], P('rep'), parts along dimension 0
- output 5: float32 [4, 1024, 4096], P('rep'), parts along dimension 0
- output 6: float32 [4, 4096, 1024], P('rep'), parts along dimension 0
- output 7: float32 [4, 1024, 4096], P('rep'), parts along dimension 0
- output 8: float32 [4, 1024, 4096], P('rep'), parts along dimension 0
- output 9: float32 [4, 4096, 1024], P('rep'), parts along dimension 0
There are 2 independent parts. A program takes and returns all parts, laid end to end along the dimension named above; an argument that names none is the same for every part.
All inputs are finite; a program needn't handle non-finite values.
Results may differ from a plain program's by a relative error of at most 0.022.
Values are sent between devices in bfloat16 or wider.
A program may use at most 2.75 GiB of HBM per device.

v0:
```python
import jax
import jax.numpy as jnp
from jax import lax
from jax.sharding import PartitionSpec as P

NAMES = ("w_gate", "w_up", "w_down")


def matmul(a, w):
    return jnp.dot(a, w, preferred_element_type=jnp.float32).astype(jnp.bfloat16)


def normed(h):
    wide = h.astype(jnp.float32)
    scale = lax.rsqrt(jnp.mean(wide**2, -1, keepdims=True) + 1e-6)
    return (wide * scale).astype(jnp.bfloat16)


def layer(h, w):
    a = normed(h)
    gate = jnp.dot(a, w["w_gate"], preferred_element_type=jnp.float32)
    up = jnp.dot(a, w["w_up"], preferred_element_type=jnp.float32)
    return h + matmul((jax.nn.silu(gate) * up).astype(jnp.bfloat16), w["w_down"])


def adamw(w, m, v, g):
    m = 0.9 * m + 0.1 * g
    v = 0.95 * v + 0.05 * g * g
    step = m * lax.rsqrt(v + 1e-8) + 0.1 * w
    return (w - 0.02 * step).astype(jnp.bfloat16), m, v


def solution(mesh):
    def step(x, dy, *arrays):
        weights, m, v = (arrays[i : i + 3] for i in (0, 3, 6))
        layers = weights[0].shape[0]
        h, kept = x[0], []
        for number in range(layers):
            kept.append(h)
            h = layer(h, {name: w[number] for name, w in zip(NAMES, weights, strict=True)})
        by_h, summed = dy[0], [None] * layers
        for number in reversed(range(layers)):
            _, back = jax.vjp(lambda w, h: layer(h, w), {name: w[number] for name, w in zip(NAMES, weights, strict=True)}, kept[number])
            by_w, by_h = back(by_h)
            summed[number] = [lax.psum(by_w[name], "dp") for name in NAMES]
        gradients = [jnp.stack([summed[number][i] for number in range(layers)]).astype(jnp.float32) for i in range(3)]
        new = [adamw(w.astype(jnp.float32), m, v, g) for w, m, v, g in zip(weights, m, v, gradients, strict=True)]
        return tuple(one[which] for which in range(3) for one in new)

    return jax.shard_map(
        step,
        mesh=mesh,
        in_specs=(P(("rep", "dp"), None, None),) * 2 + (P(None, None, None),) * 9,
        out_specs=(P("rep", None, None),) * 9,
        check_vma=False,
    )
```

profile of v0, /device:TPU:0, one launch (start us, length us, event | category | flops | bytes accessed | tf_op | source)
XLA Modules:
  0.0 1466.7 jit_solution(8674621993426858545)
XLA Ops:
  7.2 0.0 all-reduce.3.cloned.1.call-start
  7.2 6.5 copy.20
  13.8 3.1 fusion.30
  16.8 0.0 copy-start.7
  16.8 6.5 copy.21
  23.4 0.0 copy-start.4
  23.4 24.5 %convolution_convert_fusion.1 = bf16[2048,4096]{1,0:T(8,128)(2,1)} fusion(bf16[2,4096,1024]{2,1,0:T(8,128)(2,1)} %param.15, bf16[1,2048,1024]{2,1,0:T(8,128)(2,1)} %param.12), kind=kOutput, calls=%fused_computation.55 | convolution fusion | flops 17188257792 | bytes 29360128 | tf_op jit(solution)/shard_map/transpose(jvp())/dot_general | solution.py:10
  47.9 0.0 copy-done.4
  47.9 23.6 %fusion.50 = f32[2048,4096]{1,0:T(8,128)} fusion(bf16[2,1024,4096]{2,1,0:T(8,128)(2,1)} %param.13, bf16[1,2048,1024]{2,1,0:T(8,128)(2,1)S(1)} %copy-done.4, f32[2048]{0:T(1024)S(1)} %add_rsqrt_fusion), kind=kOutput, calls=%fused_computation.83 | convolution fusion | flops 17186160640 | bytes 46145536 | tf_op jit(solution)/shard_map/dot_general | solution.py:21
  71.5 0.0 copy-done.7
  71.5 38.6 %multiply_convert_fusion.1 = (bf16[2048,4096]{1,0:T(8,128)(2,1)}, f32[2048,4096]{1,0:T(8,128)}) fusion(f32[2048,4096]{1,0:T(8,128)} %fusion.50, bf16[2,1024,4096]{2,1,0:T(8,128)(2,1)} %param.14, bf16[1,2048,1024]{2,1,0:T(8,128)(2,1)} %param.11, f32[2048]{0:T(1024)S(1)} %add_rsqrt_fusion), kind=kOutput, calls=%fused_computation.44 | convolution fusion | flops 17236492288 | bytes 96477184 | tf_op jit(solution)/shard_map/dot_general | solution.py:22
  110.0 23.5 %fusion.34 = (f32[2048]{0:T(1024)S(1)}, bf16[2048,1024]{0,1:T(8,128)(2,1)S(1)}) fusion(bf16[2048,4096]{1,0:T(8,128)(2,1)} %get-tuple-element.24, bf16[2,4096,1024]{2,1,0:T(8,128)(2,1)} %param.15, bf16[1,2048,1024]{1,2,0:T(8,128)(2,1)} %copy.20), kind=kOutput, calls=%fused_computation.67 | convolution fusion | flops 17190352896 | bytes 33562624 | tf_op jit(solution)/shard_map/dot_general | solution.py:10
  133.6 0.0 copy-start.5
  133.6 0.0 copy-start.2
  133.6 0.6 copy-done.5
  134.2 1.4 copy-done.2
  135.5 23.6 %fusion.37 = f32[2048,4096]{1,0:T(8,128)} fusion(bf16[2,1024,4096]{2,1,0:T(8,128)(2,1)} %param.14, bf16[2048,1024]{0,1:T(8,128)(2,1)S(1)} %get-tuple-element.27, f32[2048]{0:T(1024)S(1)} %fusion.80), kind=kOutput, calls=%fused_computation.70 | convolution fusion | flops 17186160640 | bytes 46145536 | tf_op jit(solution)/shard_map/jvp()/dot_general | solution.py:22
  159.1 46.6 %fusion.14 = (bf16[2048,4096]{1,0:T(8,128)(2,1)}, f32[2048,4096]{1,0:T(8,128)}) fusion(f32[2048,4096]{1,0:T(8,128)} %fusion.37, bf16[2048,4096]{1,0:T(8,128)(2,1)} %convolution_convert_fusion.1, bf16[2,1024,4096]{2,1,0:T(8,128)(2,1)} %param.13, bf16[2048,1024]{0,1:T(8,128)(2,1)} %copy-done.2, f32[2048]{0:T(1024)S(1)} %fusion.80), kind=kOutput, calls=%fused_computation.32 | convolution fusion | flops 17286823936 | bytes 113254400 | tf_op jit(solution)/shard_map/jvp()/dot_general | solution.py:21
  205.7 27.1 %fusion.27 = bf16[2048,1024]{0,1:T(8,128)(2,1)} fusion(bf16[2048,4096]{1,0:T(8,128)(2,1)} %convolution_convert_fusion.1, bf16[2,1024,4096]{2,1,0:T(8,128)(2,1)} %param.14, f32[2048,4096]{1,0:T(8,128)} %get-tuple-element.29), kind=kOutput, calls=%fused_computation.48 | convolution fusion | flops 17230200832 | bytes 62914560 | tf_op jit(solution)/shard_map/transpose(jvp())/dot_general | solution.py:22
  232.9 26.7 %convert_bitcast_fusion.2 = bf16[1,1024,4096]{2,1,0:T(8,128)(2,1)} fusion(bf16[2048,4096]{1,0:T(8,128)(2,1)} %convolution_convert_fusion.1, bf16[2048,1024]{0,1:T(8,128)(2,1)} %copy-done.2, f32[2048]{0:T(1024)S(1)} %fusion.80, f32[2048,4096]{1,0:T(8,128)} %get-tuple-element.29), kind=kOutput, calls=%fused_computation.87 | convolution fusion | flops 17240686592 | bytes 62922752 | tf_op jit(solution)/shard_map/transpose(jvp())/dot_general | solution.py:22
  259.5 0.0 copy-start.3
  259.5 30.9 %convert_bitcast_fusion = bf16[1,4096,1024]{2,1,0:T(8,128)(2,1)} fusion(f32[2048,4096]{1,0:T(8,128)} %fusion.37, bf16[1,2048,1024]{2,1,0:T(8,128)(2,1)} %param.12, f32[2048,4096]{1,0:T(8,128)} %get-tuple-element.29), kind=kOutput, calls=%fused_computation.85 | convolution fusion | flops 17234395136 | bytes 79691776 | tf_op jit(solution)/shard_map/transpose(jvp())/dot_general | solution.py:10
  290.5 0.0 copy-done.3
  290.5 21.6 %convert_bitcast_fusion.4 = bf16[1,1024,4096]{2,1,0:T(8,128)(2,1)} fusion(bf16[2048,4096]{1,0:T(8,128)(2,1)} %get-tuple-element.28, bf16[2048,1024]{0,1:T(8,128)(2,1)S(1)} %copy-done.3, f32[2048]{0:T(1024)S(1)} %fusion.80), kind=kOutput, calls=%fused_computation.89 | convolution fusion | flops 17186160640 | bytes 29368320 | tf_op jit(solution)/shard_map/transpose(jvp())/dot_general | solution.py:21
  312.1 0.0 copy-start.6
  312.1 0.0 copy-start
  312.1 25.4 %fusion.36 = (f32[2048]{0:T(1024)S(1)}, bf16[2048,1024]{0,1:T(8,128)(2,1)}) fusion(bf16[2048,1024]{0,1:T(8,128)(2,1)S(1)} %copy-done.3, bf16[2048,1024]{0,1:T(8,128)(2,1)} %fusion.27, bf16[2048,4096]{1,0:T(8,128)(2,1)} %get-tuple-element.28, bf16[2,1024,4096]{2,1,0:T(8,128)(2,1)} %param.13), kind=kOutput, calls=%fused_computation.69 | convolution fusion | flops 17190352896 | bytes 37756928 | tf_op jit(solution)/shard_map/transpose(jvp())/dot_general | solution.py:21
  337.5 0.0 copy-done.6
  337.5 0.0 copy-done
  337.5 6.0 fusion.65
  343.5 25.0 %convolution_convert_fusion = bf16[2048,4096]{1,0:T(8,128)(2,1)} fusion(bf16[2048,1024]{0,1:T(8,128)(2,1)} %fusion.65, bf16[2,4096,1024]{2,1,0:T(8,128)(2,1)} %param.15), kind=kOutput, calls=%fused_computation.54 | convolution fusion | flops 17188257792 | bytes 29360128 | tf_op jit(solution)/shard_map/transpose(jvp())/dot_general | solution.py:10
  368.5 0.0 copy-start.1
  368.5 0.0 copy-start.8
  368.5 24.4 %convert_bitcast_fusion.1 = bf16[1,4096,1024]{2,1,0:T(8,128)(2,1)} fusion(bf16[2048,4096]{1,0:T(8,128)(2,1)} %get-tuple-element.24, bf16[2048,1024]{0,1:T(8,128)(2,1)} %fusion.65), kind=kOutput, calls=%fused_computation.86 | convolution fusion | flops 17184063488 | bytes 29360128 | tf_op jit(solution)/shard_map/transpose(jvp())/dot_general | solution.py:10
  392.9 0.0 copy-done.1
  392.9 0.0 copy-done.8
  392.9 25.5 %convert_bitcast_fusion.3 = bf16[1,1024,4096]{2,1,0:T(8,128)(2,1)} fusion(bf16[2048,4096]{1,0:T(8,128)(2,1)} %convolution_convert_fusion, f32[2048,4096]{1,0:T(8,128)} %fusion.50, bf16[1,2048,1024]{1,2,0:T(8,128)(2,1)S(1)} %copy-done.1, f32[2048]{0:T(1024)S(1)} %copy-done.8), kind=kOutput, calls=%fused_computation.88 | convolution fusion | flops 17240686592 | bytes 62922752 | tf_op jit(solution)/shard_map/transpose(jvp())/dot_general | solution.py:22
  418.4 37.1 %convert_bitcast_fusion.5 = bf16[1,1024,4096]{2,1,0:T(8,128)(2,1)} fusion(f32[2048,4096]{1,0:T(8,128)} %fusion.50, f32[2048,4096]{1,0:T(8,128)} %get-tuple-element.25, bf16[2048,4096]{1,0:T(8,128)(2,1)} %convolution_convert_fusion, bf16[1,2048,1024]{1,2,0:T(8,128)(2,1)} %copy.20, f32[2048]{0:T(1024)S(1)} %copy-done.8), kind=kOutput, calls=%fused_computation.90 | convolution fusion | flops 17282629632 | bytes 96477184 | tf_op jit(solution)/shard_map/transpose(jvp())/dot_general | solution.py:21
  455.5 0.0 all-reduce.3.cloned.1.call-update
  455.5 830.0 %all-reduce.3.cloned.1.call-done = (bf16[1,1024,4096]{2,1,0:T(8,128)(2,1)}, bf16[1,1024,4096]{2,1,0:T(8,128)(2,1)}, bf16[1,1024,4096]{2,1,0:T(8,128)(2,1)}, bf16...) async-done(((bf16[1,1024,4096]{2,1,0:T(8,128)(2,1)}, bf16[1,1024,4096]{2,1,0:T(8,128)(2,1)}, ...) | async-done | bytes 50331664 | tf_op jit(solution)/shard_map/psum | solution.py:45
  1285.6 57.5 %fusion.11 = (bf16[2,4096,1024]{2,1,0:T(8,128)(2,1)}, f32[2,4096,1024]{2,1,0:T(8,128)}, f32[2,4096,1024]{2,1,0:T(8,128)}) fusion(bf16[2,4096,1024]{2,1,0:T(8,128)(2,1)} %param.15, bf16[1,4096,1024]{2,1,0:T(8,128)(2,1)} %get-tuple-element.13, bf16[1,4096,1024]{2,1,0:T(8,128)(2,1)} %get-tuple-element.14, f32[2,4096,1024]{2,1,0:T(8,128)} %param.21, ...), kind=kLoop, calls=%fused_computation.29 | loop fusion | flops 159383552 | bytes 184549376 | tf_op jit(solution)/shard_map/convert_element_type | solution.py:30
  1343.1 116.2 %fusion.2 = (bf16[2,1024,4096]{2,1,0:T(8,128)(2,1)}, f32[2,1024,4096]{2,1,0:T(8,128)}, f32[2,1024,4096]{2,1,0:T(8,128)}, bf16[2,1024,4096]{2,1,0:T(8,128)(2,1)},...) fusion(bf16[2,1024,4096]{2,1,0:T(8,128)(2,1)} %param.13, bf16[1,1024,4096]{2,1,0:T(8,128)(2,1)} %get-tuple-element.9, ...), kind=kLoop, calls=%fused_computation.20 | loop fusion | flops 318767104 | bytes 369098752 | tf_op jit(solution)/shard_map/convert_element_type | solution.py:30
  (3 shorter events, 0.0 us)
Async XLA Ops:
  7.2 1278.4 %all-reduce.3.cloned.1.call-start = ((), (), s32[]{:S(2)}) async-start(), calls=%async_computation | async-start | bytes 100663296 | tf_op jit(solution)/shard_map/psum | solution.py:45
  16.8 54.6 %copy-start.7 = (f32[2048]{0:T(1024)}, f32[2048]{0:T(1024)S(1)}, u32[]{:S(2)}) copy-start(f32[2048]{0:T(1024)S(1)} %add_rsqrt_fusion) | copy-start | bytes 24580
  23.4 24.5 %copy-start.4 = (bf16[1,2048,1024]{2,1,0:T(8,128)(2,1)S(1)}, bf16[1,2048,1024]{2,1,0:T(8,128)(2,1)}, u32[]{:S(2)}) copy-start(bf16[1,2048,1024]{2,1,0:T(8,128)(2,1)} %param.11) | copy-start | bytes 12582916
  133.6 0.6 copy-start.5
  133.6 2.0 copy-start.2
  259.5 30.9 %copy-start.3 = (bf16[2048,1024]{0,1:T(8,128)(2,1)S(1)}, bf16[2048,1024]{0,1:T(8,128)(2,1)}, u32[]{:S(2)}) copy-start(bf16[2048,1024]{0,1:T(8,128)(2,1)} %copy-done.2) | copy-start | bytes 12582916
  312.1 25.4 %copy-start.6 = (f32[2048]{0:T(1024)S(1)}, f32[2048]{0:T(1024)}, u32[]{:S(2)}) copy-start(f32[2048]{0:T(1024)} %copy-done.5) | copy-start | bytes 24580
  312.1 25.4 %copy-start = (bf16[1,2048,1024]{1,2,0:T(8,128)(2,1)S(1)}, bf16[1,2048,1024]{1,2,0:T(8,128)(2,1)}, u32[]{:S(2)}) copy-start(bf16[1,2048,1024]{1,2,0:T(8,128)(2,1)} %copy.21) | copy-start | bytes 12582916
  368.5 24.4 %copy-start.1 = (bf16[1,2048,1024]{1,2,0:T(8,128)(2,1)S(1)}, bf16[1,2048,1024]{1,2,0:T(8,128)(2,1)}, u32[]{:S(2)}) copy-start(bf16[1,2048,1024]{1,2,0:T(8,128)(2,1)} %copy.20) | copy-start | bytes 12582916
  368.5 24.4 %copy-start.8 = (f32[2048]{0:T(1024)S(1)}, f32[2048]{0:T(1024)}, u32[]{:S(2)}) copy-start(f32[2048]{0:T(1024)} %copy-done.7) | copy-start | bytes 24580
Sparse Core Ops, SparseCore 0:
  455.7 829.8 all-reduce.2
where the time goes:
time: 1470 us
  waiting for transfers between devices  830 us (56%)
  matrix products  424 us (29%)
  other arithmetic  183 us (12%)
  local copies, waits for them, and re-layouts  15 us (1%)
    psum x1, waiting for transfers between devices, step(): summed[number] = [lax.psum(by_w[name], 'dp') for name in NAMES]  830 us
    convert_element_type x2, other arithmetic, adamw(): return ((w - 0.02 * step).astype(jnp.bfloat16), m, v)  174 us
    dot_general x5, matrix products, layer(): gate = jnp.dot(a, w['w_gate'], preferred_element_type=jnp.float32)  154 us
    dot_general x5, matrix products, layer(): up = jnp.dot(a, w['w_up'], preferred_element_type=jnp.float32)  141 us
    dot_general x5, matrix products, matmul(): jnp.dot(a, w, preferred_element_type=jnp.float32).astype(jnp.bfloat16)  128 us
  transfers between devices with their start and end apart: 1, of which 1 were waited for; matrix products, arithmetic and copies ran while one was open for 0% of the time, Pallas kernels for 0%

commit v1 on v0

v1 whole, which is shorter than its diff:
```python
import jax
import jax.numpy as jnp
from jax import lax
from jax.experimental import pallas as pl
from jax.experimental.pallas import tpu as pltpu
from jax.sharding import PartitionSpec as P


CHIPS = 8


def dot(a, b, over):
    return lax.dot_general(a, b, (((over[0],), (over[1],)), ((), ())), preferred_element_type=jnp.float32)


def normed(h):
    wide = h.astype(jnp.float32)
    scale = lax.rsqrt(jnp.mean(wide**2, -1, keepdims=True) + 1e-6)
    return (wide * scale).astype(jnp.bfloat16)


def device_at(place, core):
    place = place if core == 0 else CHIPS - 1 - place
    y, z = (0, place) if place < CHIPS // 2 else (1, CHIPS - 1 - place)
    return (y * (CHIPS // 2) + z) * 2 + core


NEXT = [(device_at(q, core), device_at((q + 1) % CHIPS, core)) for core in range(2) for q in range(CHIPS)]
BACK = [(to, of) for of, to in NEXT]
SWAP = [(d, d ^ 1) for d in range(2 * CHIPS)]


def where_am_i():
    index = lax.axis_index("dp")
    core = index % 2
    chip = index // 2
    z, y = chip % (CHIPS // 2), chip // (CHIPS // 2)
    place = jnp.where(y == 0, z, CHIPS - 1 - z)
    return core, jnp.where(core == 0, place, CHIPS - 1 - place)


def take(array, index):
    return lax.dynamic_index_in_dim(array, index, 0, keepdims=False)


def permuted(array, pairs):
    return lax.ppermute(array, "dp", pairs)


PARTS = ((0, -1, 1, -2, 2), (-3, 3, -4))


def summed_over_group(g, core, q):
    rows, columns = g.shape
    g = g.reshape(2, CHIPS, rows // (2 * CHIPS), columns)
    own = take(g, core)
    other = permuted(take(g, 1 - core), SWAP)

    def local(ahead):
        chunk = (q + CHIPS + ahead) % CHIPS
        return take(own, chunk).astype(jnp.float32) + take(other, chunk).astype(jnp.float32)

    half = CHIPS // 2
    right, left = local(half), None
    for stage in range(1, half + 1):
        right = permuted(right.astype(jnp.bfloat16), NEXT).astype(jnp.float32)
        if stage == 1:
            left = local(1 - half)
        else:
            left = permuted(left.astype(jnp.bfloat16), BACK).astype(jnp.float32)
        if stage < half:
            right = right + local(half - stage)
            if stage > 1:
                left = left + local(stage - half)
    final = (right + left + local(0)).astype(jnp.bfloat16)
    behind, ahead = [final], [final]
    for stage in range(1, half + 1):
        behind.append(permuted(behind[-1], NEXT))
        if stage < half:
            ahead.append(permuted(ahead[-1], BACK))
    for order in PARTS:
        mine = jnp.stack([behind[-n] if n <= 0 else ahead[n] for n in order])
        yield order, mine, permuted(mine, SWAP)


def adamw_kernel(at, order, w, m, v, mine, theirs, *rest):
    new_w, new_m, new_v = rest[-3:]
    g = jnp.where(pl.program_id(0) == 0, mine[0].astype(jnp.float32), theirs[0].astype(jnp.float32))
    m = 0.9 * m[0] + 0.1 * g
    v = 0.95 * v[0] + 0.05 * g * g
    wide = w[0].astype(jnp.float32)
    step = m * lax.rsqrt(v + 1e-8) + 0.1 * wide
    new_w[0] = (wide - 0.02 * step).astype(jnp.bfloat16)
    new_m[0] = m
    new_v[0] = v


def adamw(number, w, m, v, mine, theirs, at, order, so_far):
    _, rows, columns = w.shape
    block = rows // (2 * CHIPS)
    chunks = len(order)
    order = jnp.array(order, jnp.int32)

    def place(t, s, at, order):
        half = jnp.where(t == 0, at[0], 1 - at[0])
        q = jnp.where(t == 0, at[1], CHIPS - 1 - at[1])
        return number, half * CHIPS + lax.rem(q + CHIPS + order[s], CHIPS), 0

    spec = pl.BlockSpec((1, block, columns), place)
    in_specs = [
        spec,
        spec,
        spec,
        pl.BlockSpec((1, block, columns), lambda t, s, at, order: (jnp.where(t == 0, s, chunks - 1), 0, 0)),
        pl.BlockSpec((1, block, columns), lambda t, s, at, order: (jnp.where(t == 0, 0, s), 0, 0)),
    ] + [pl.BlockSpec(memory_space=pl.ANY)] * len(so_far)
    return pl.pallas_call(
        adamw_kernel,
        grid_spec=pltpu.PrefetchScalarGridSpec(
            num_scalar_prefetch=2, grid=(2, chunks), in_specs=in_specs, out_specs=[spec] * 3
        ),
        out_shape=[jax.ShapeDtypeStruct(w.shape, dtype) for dtype in (jnp.bfloat16, jnp.float32, jnp.float32)],
        input_output_aliases={7 + i: i for i in range(len(so_far))},
        compiler_params=pltpu.CompilerParams(
            dimension_semantics=("arbitrary", "arbitrary"), vmem_limit_bytes=32 * 2**20
        ),
        cost_estimate=pl.CostEstimate(
            flops=40 * chunks * block * columns,
            bytes_accessed=44 * chunks * block * columns,
            transcendentals=2 * chunks * block * columns,
        ),
    )(at, order, w, m, v, mine, theirs, *so_far)


def solution(mesh):
    def whole(x, dy, *arrays):
        weights, m, v = (arrays[i : i + 3] for i in (0, 3, 6))
        layers = weights[0].shape[0]
        core, q = where_am_i()
        at = jnp.stack([core, q]).astype(jnp.int32)
        h, kept = x[0], []
        for number in range(layers):
            w_gate, w_up, w_down = (w[number] for w in weights)
            a, back = jax.vjp(normed, h)
            gate, up = dot(a, w_gate, (1, 0)), dot(a, w_up, (1, 0))
            act = (jax.nn.silu(gate) * up).astype(jnp.bfloat16)
            gate, up, act = lax.optimization_barrier((gate, up, act))
            kept.append((a, gate, up, act, back))
            if number < layers - 1:
                h = h + dot(act, w_down, (1, 0)).astype(jnp.bfloat16)
        by_h, new = dy[0], [()] * 3
        for number in reversed(range(layers)):
            w_gate, w_up, w_down = (w[number] for w in weights)
            a, gate, up, act, back = kept[number]

            def take_step(i, g):
                for order, mine, theirs in summed_over_group(g, core, q):
                    new[i] = adamw(number, weights[i], m[i], v[i], mine, theirs, at, order, new[i])

            g = dot(act, by_h, (0, 0)).astype(jnp.bfloat16)
            take_step(2, g)
            by_act = dot(by_h, w_down, (1, 1)).astype(jnp.bfloat16).astype(jnp.float32)
            gated, back_silu = jax.vjp(jax.nn.silu, gate)
            by_up = (by_act * gated).astype(jnp.bfloat16)
            by_gate = back_silu(by_act * up)[0].astype(jnp.bfloat16)
            by_gate, by_up = lax.optimization_barrier((by_gate, by_up))
            g = dot(a, by_gate, (0, 0)).astype(jnp.bfloat16)
            take_step(0, g)
            g = dot(a, by_up, (0, 0)).astype(jnp.bfloat16)
            take_step(1, g)
            if number:
                by_a = dot(by_gate, w_gate, (1, 1)).astype(jnp.bfloat16)
                by_a = lax.optimization_barrier(by_a)
                by_a = by_a + dot(by_up, w_up, (1, 1)).astype(jnp.bfloat16)
                by_a = lax.optimization_barrier(by_a)
                by_h = by_h + back(by_a)[0]
        return tuple(one[which] for which in range(3) for one in new)

    return jax.shard_map(
        whole,
        mesh=mesh,
        in_specs=(P(("rep", "dp"), None, None),) * 2 + (P(None, None, None),) * 9,
        out_specs=(P("rep", None, None),) * 9,
        check_vma=False,
    )
```

time: 1470 us -> 1220 us (0.83)
  waiting for transfers between devices: 830 us -> 326 us
  Pallas kernels: 0 us -> 207 us
  starting transfers between devices: 0.04 us -> 119 us
  other arithmetic: 183 us -> 73.6 us
  local copies, waits for them, and re-layouts: 15 us -> 70.8 us
    psum x1 -> x0, waiting for transfers between devices: 830 us -> none  [step(): summed[number] = [lax.psum(by_w[name], 'dp') for name in NAMES]]
    ppermute x0 -> x102, waiting for transfers between devices: none -> 326 us  [permuted(): return lax.ppermute(array, 'dp', pairs)]
    pallas_call x0 -> x12, Pallas kernels: none -> 207 us  [adamw(): pl.pallas_call(adamw_kernel, grid_spec=pltpu.PrefetchScalarGridSpec(num_s...]
    convert_element_type x2 -> x24, other arithmetic: 174 us -> 44.1 us  [summed_over_group(): right = permuted(right.astype(jnp.bfloat16), NEXT).astype(jnp.float32)]
    ppermute x0 -> x102, starting transfers between devices: none -> 119 us  [permuted(): return lax.ppermute(array, 'dp', pairs)]
    unnamed x20 -> x122, local copies, waits for them, and re-layouts: 15 us -> 51.4 us
    squeeze x0 -> x6, local copies, waits for them, and re-layouts: none -> 17.1 us  [take(): return lax.dynamic_index_in_dim(array, index, 0, keepdims=False)]
  transfers between devices with their start and end apart: 1 -> 102, of which waited for: 1 -> 48; matrix products, arithmetic and copies ran while one was open for 0% -> 28% of each run, Pallas kernels for 0% -> 16%
where the time goes in v1:
time: 1220 us; the launch traced here: 1210 us
  matrix products  412 us (34%)
  waiting for transfers between devices  326 us (27%)
  Pallas kernels  207 us (17%)
  starting transfers between devices  119 us (10%)
  other arithmetic  73.6 us (6%)
  local copies, waits for them, and re-layouts  70.8 us (6%)
    dot_general x15, matrix products, dot(): lax.dot_general(a, b, (((over[0],), (over[1],)), ((), ())), preferred_ele...  412 us
    ppermute x102, waiting for transfers between devices, permuted(): return lax.ppermute(array, 'dp', pairs)  326 us
    pallas_call x12, Pallas kernels, adamw(): pl.pallas_call(adamw_kernel, grid_spec=pltpu.PrefetchScalarGridSpec(num_s...  207 us
    ppermute x102, starting transfers between devices, permuted(): return lax.ppermute(array, 'dp', pairs)  119 us
    unnamed x122, local copies, waits for them, and re-layouts  51.4 us
    convert_element_type x24, other arithmetic, summed_over_group(): right = permuted(right.astype(jnp.bfloat16), NEXT).astype(jnp.float32)  44.1 us
  transfers between devices with their start and end apart: 102, of which 48 were waited for; matrix products, arithmetic and copies ran while one was open for 28% of the time, Pallas kernels for 16%

profile of v1, /device:TPU:0, one launch (start us, length us, event | category | flops | bytes accessed | tf_op | source)
XLA Modules:
  0.0 1210.9 jit_solution(9989086649551179079)
XLA Ops:
  0.7 6.5 copy.59
  10.3 24.6 %fusion.28 = f32[2048,4096]{1,0:T(8,128)} fusion(bf16[2,1024,4096]{2,1,0:T(8,128)(2,1)} %w.15, bf16[1,2048,1024]{2,1,0:T(8,128)(2,1)} %param.23, f32[2048]{0:T(1024)S(1)} %add_rsqrt_fusion), kind=kOutput, calls=%fused_computation.47 | convolution fusion | flops 17186160640 | bytes 46145536 | tf_op jit(solution)/shard_map/dot_general | solution.py:13
  34.8 38.0 %multiply_convert_fusion.1 = (bf16[2048,4096]{1,0:T(8,128)(2,1)}, f32[2048,4096]{1,0:T(8,128)}) fusion(f32[2048,4096]{1,0:T(8,128)} %fusion.28, bf16[2,1024,4096]{2,1,0:T(8,128)(2,1)} %w.19, bf16[1,2048,1024]{2,1,0:T(8,128)(2,1)} %param.23, f32[2048]{0:T(1024)S(1)} %add_rsqrt_fusion), kind=kOutput, calls=%fused_computation.17 | convolution fusion | flops 17236492288 | bytes 96477184 | tf_op jit(solution)/shard_map/dot_general | solution.py:13
  72.8 24.0 %fusion.12 = (f32[2048]{0:T(1024)S(1)}, bf16[2048,1024]{0,1:T(8,128)(2,1)S(1)}) fusion(bf16[2048,4096]{1,0:T(8,128)(2,1)} %get-tuple-element.55, bf16[2,4096,1024]{2,1,0:T(8,128)(2,1)} %w.23, bf16[1,2048,1024]{1,2,0:T(8,128)(2,1)} %copy.59), kind=kOutput, calls=%fused_computation.31 | convolution fusion | flops 17190352896 | bytes 33562624 | tf_op jit(solution)/shard_map/dot_general | solution.py:13
  98.9 23.4 %fusion.21 = f32[2048,4096]{1,0:T(8,128)} fusion(bf16[2,1024,4096]{2,1,0:T(8,128)(2,1)} %w.15, bf16[2048,1024]{0,1:T(8,128)(2,1)S(1)} %get-tuple-element.156, f32[2048]{0:T(1024)S(1)} %fusion.143), kind=kOutput, calls=%fused_computation.40 | convolution fusion | flops 17186160640 | bytes 46145536 | tf_op jit(solution)/shard_map/dot_general | solution.py:13
  122.3 39.2 %multiply_convert_fusion = (bf16[2048,4096]{1,0:T(8,128)(2,1)}, f32[2048,4096]{1,0:T(8,128)}) fusion(f32[2048,4096]{1,0:T(8,128)} %fusion.21, bf16[2,1024,4096]{2,1,0:T(8,128)(2,1)} %w.19, bf16[2048,1024]{0,1:T(8,128)(2,1)} %copy-done.22, f32[2048]{0:T(1024)S(1)} %fusion.143), kind=kOutput, calls=%fused_computation.16 | convolution fusion | flops 17236492288 | bytes 96477184 | tf_op jit(solution)/shard_map/dot_general | solution.py:13
  161.5 21.9 %convolution_convert_fusion.2 = bf16[4096,1024]{1,0:T(8,128)(2,1)S(1)} fusion(bf16[2048,4096]{1,0:T(8,128)(2,1)} %get-tuple-element.84, bf16[1,2048,1024]{2,1,0:T(8,128)(2,1)} %param.24), kind=kOutput, calls=%fused_computation.54 | convolution fusion | flops 17184063488 | bytes 29360128 | tf_op jit(solution)/shard_map/dot_general | solution.py:13
  189.7 44.5 %fusion = (bf16[2048,4096]{1,0:T(8,128)(2,1)}, bf16[2048,4096]{1,0:T(8,128)(2,1)}) fusion(f32[2048,4096]{1,0:T(8,128)} %fusion.21, f32[2048,4096]{1,0:T(8,128)} %get-tuple-element.56, bf16[2,4096,1024]{2,1,0:T(8,128)(2,1)} %w.23, bf16[1,2048,1024]{2,1,0:T(8,128)(2,1)} %param.24), kind=kOutput, calls=%fused_computation.6 | convolution fusion | flops 17314086912 | bytes 113246208 | tf_op jit(solution)/shard_map/dot_general | solution.py:13
  234.2 21.5 %convolution_convert_fusion.6 = bf16[1024,4096]{1,0:T(8,128)(2,1)S(1)} fusion(bf16[2048,4096]{1,0:T(8,128)(2,1)} %get-tuple-element.58, bf16[2048,1024]{0,1:T(8,128)(2,1)} %copy-done.22, f32[2048]{0:T(1024)S(1)} %fusion.143), kind=kOutput, calls=%fused_computation.58 | convolution fusion | flops 17190354944 | bytes 29368320 | tf_op jit(solution)/shard_map/dot_general | solution.py:13
  261.4 20.3 %convolution_convert_fusion.4 = bf16[1024,4096]{1,0:T(8,128)(2,1)S(1)} fusion(bf16[2048,4096]{1,0:T(8,128)(2,1)} %get-tuple-element.59, bf16[2048,1024]{0,1:T(8,128)(2,1)S(1)} %copy-done.23, f32[2048]{0:T(1024)S(1)} %fusion.143), kind=kOutput, calls=%fused_computation.56 | convolution fusion | flops 17190354944 | bytes 29368320 | tf_op jit(solution)/shard_map/dot_general | solution.py:13
  288.1 6.5 copy.60
  294.6 24.2 %fusion.46 = bf16[2048,1024]{0,1:T(8,128)(2,1)} fusion(bf16[2048,4096]{1,0:T(8,128)(2,1)} %get-tuple-element.58, bf16[2,1024,4096]{2,1,0:T(8,128)(2,1)} %w.15), kind=kOutput, calls=%fused_computation.78 | convolution fusion | flops 17181966336 | bytes 29360128 | tf_op jit(solution)/shard_map/dot_general | solution.py:13
  318.8 23.3 %convert_add_fusion = bf16[2048,1024]{0,1:T(8,128)(2,1)S(1)} fusion(bf16[2048,1024]{0,1:T(8,128)(2,1)} %fusion.46, bf16[2048,4096]{1,0:T(8,128)(2,1)} %get-tuple-element.59, bf16[2,1024,4096]{2,1,0:T(8,128)(2,1)} %w.19), kind=kOutput, calls=%fused_computation.77 | convolution fusion | flops 17184063488 | bytes 33554432 | tf_op jit(solution)/shard_map/dot_general | solution.py:13
  348.8 24.4 %convolution_convert_fusion.3 = bf16[4096,1024]{1,0:T(8,128)(2,1)} fusion(bf16[2048,4096]{1,0:T(8,128)(2,1)} %get-tuple-element.55, bf16[2048,1024]{0,1:T(8,128)(2,1)} %fusion.41), kind=kOutput, calls=%fused_computation.55 | convolution fusion | flops 17184063488 | bytes 29360128 | tf_op jit(solution)/shard_map/dot_general | solution.py:13
  377.8 42.7 %fusion.1 = (bf16[2048,4096]{1,0:T(8,128)(2,1)}, bf16[2048,4096]{1,0:T(8,128)(2,1)}) fusion(f32[2048,4096]{1,0:T(8,128)} %fusion.28, f32[2048,4096]{1,0:T(8,128)} %get-tuple-element.60, bf16[2048,1024]{0,1:T(8,128)(2,1)} %fusion.41, bf16[2,4096,1024]{2,1,0:T(8,128)(2,1)S(1)} %bitcast.480), kind=kOutput, calls=%fused_computation.7 | convolution fusion | flops 17314086912 | bytes 113246208 | tf_op jit(solution)/shard_map/dot_general | solution.py:13
  420.4 21.9 %convolution_convert_fusion.5 = bf16[1024,4096]{1,0:T(8,128)(2,1)S(1)} fusion(bf16[2048,4096]{1,0:T(8,128)(2,1)} %get-tuple-element.73, bf16[1,2048,1024]{1,2,0:T(8,128)(2,1)} %copy.59, f32[2048]{0:T(1024)S(1)} %copy-done.41), kind=kOutput, calls=%fused_computation.57 | convolution fusion | flops 17190354944 | bytes 29368320 | tf_op jit(solution)/shard_map/dot_general | solution.py:13
  448.4 18.6 %convolution_convert_fusion.7 = bf16[1024,4096]{1,0:T(8,128)(2,1)S(1)} fusion(bf16[2048,4096]{1,0:T(8,128)(2,1)S(1)} %copy-done.42, bf16[1,2048,1024]{1,2,0:T(8,128)(2,1)S(1)} %copy-done.26, f32[2048]{0:T(1024)S(1)} %copy-done.41), kind=kOutput, calls=%fused_computation.59 | convolution fusion | flops 17190354944 | bytes 29368320 | tf_op jit(solution)/shard_map/dot_general | solution.py:13
  499.6 13.0 %collective-permute-done.35 = bf16[64,4096]{1,0:T(8,128)(2,1)S(1)} collective-permute-done((bf16[64,4096]{1,0:T(8,128)(2,1)S(1)}, bf16[64,4096]{1,0:T(8,128)(2,1)S(1)}, u32[]{:S(2)}, u32[]{:S(2)}) %collective-permute-start.35) | collective-permute-done | bytes 524320 | tf_op jit(solution)/shard_map/ppermute | solution.py:47
  524.3 10.8 collective-permute-done.19
  568.7 6.4 collective-permute-done.2
  577.6 9.6 collective-permute-done.5
  608.6 15.2 %collective-permute-done.57 = bf16[64,4096]{1,0:T(8,128)(2,1)S(1)} collective-permute-done((bf16[64,4096]{1,0:T(8,128)(2,1)S(1)}, bf16[64,4096]{1,0:T(8,128)(2,1)S(1)}, u32[]{:S(2)}, u32[]{:S(2)}) %collective-permute-start.57) | collective-permute-done | bytes 524320 | tf_op jit(solution)/shard_map/ppermute | solution.py:47
  645.2 15.9 %collective-permute-done.6 = bf16[64,4096]{1,0:T(8,128)(2,1)S(1)} collective-permute-done((bf16[64,4096]{1,0:T(8,128)(2,1)S(1)}, bf16[64,4096]{1,0:T(8,128)(2,1)S(1)}, u32[]{:S(2)}, u32[]{:S(2)}) %collective-permute-start.6) | collective-permute-done | bytes 524320 | tf_op jit(solution)/shard_map/ppermute | solution.py:47
  682.5 15.9 %collective-permute-done.58 = bf16[64,4096]{1,0:T(8,128)(2,1)S(1)} collective-permute-done((bf16[64,4096]{1,0:T(8,128)(2,1)S(1)}, bf16[64,4096]{1,0:T(8,128)(2,1)S(1)}, u32[]{:S(2)}, u32[]{:S(2)}) %collective-permute-start.58) | collective-permute-done | bytes 524320 | tf_op jit(solution)/shard_map/ppermute | solution.py:47
  719.3 11.6 collective-permute-done.7
  739.5 6.8 collective-permute-done.25
  762.0 11.3 collective-permute-done.42
  776.7 10.8 collective-permute-done.45
  787.6 14.6 %collective-permute-done.8 = bf16[64,4096]{1,0:T(8,128)(2,1)S(1)} collective-permute-done((bf16[64,4096]{1,0:T(8,128)(2,1)S(1)}, bf16[64,4096]{1,0:T(8,128)(2,1)S(1)}, u32[]{:S(2)}, u32[]{:S(2)}) %collective-permute-start.8) | collective-permute-done | bytes 524320 | tf_op jit(solution)/shard_map/ppermute | solution.py:47
  806.7 9.8 collective-permute-done.11
  823.1 9.9 collective-permute-done.29
  835.3 9.0 collective-permute-done.63
  849.9 22.5 %collective-permute-done.80 = bf16[256,1024]{1,0:T(8,128)(2,1)S(1)} collective-permute-done((bf16[256,1024]{1,0:T(8,128)(2,1)S(1)}, bf16[256,1024]{1,0:T(8,128)(2,1)S(1)}, u32[]{:S(2)}, u32[]{:S(2)}) %collective-permute-start.80) | collective-permute-done | bytes 524320 | tf_op jit(solution)/shard_map/ppermute | solution.py:47
  876.6 10.5 collective-permute-done.9
  889.1 9.3 collective-permute-done.98
  924.3 7.7 collective-permute-done.31
  991.8 20.9 %shard_map.290 = (bf16[2,1024,4096]{2,1,0:T(8,128)(2,1)}, f32[2,1024,4096]{2,1,0:T(8,128)}, f32[2,1024,4096]{2,1,0:T(8,128)}) custom-call(s32[2]{0:T(128)S(1)} %pad_add_fusion.at, s32[5]{0:T(128)S(1)} %copy-done.21, bf16[2,1024,4096]{2,1,0:T(8,128)(2,1)S(1)} %bitcast.478, f32[2,1024,4096]{2,1,0:T(8,128)} %m.19, f32[2,1024,4096]{2,1,0:T(8,128)} %v.19, ...), custom_call_target="tpu_custom_call" | custom-call | flops 52428800 | bytes 57671680 | tf_op jit(solution)/shard_map/pallas_call | solution.py:117
  1012.8 13.1 %shard_map.291 = (bf16[2,1024,4096]{2,1,0:T(8,128)(2,1)}, f32[2,1024,4096]{2,1,0:T(8,128)}, f32[2,1024,4096]{2,1,0:T(8,128)}) custom-call(s32[2]{0:T(128)S(1)} %pad_add_fusion.at, s32[3]{0:T(128)S(1)} %copy-done.20, bf16[2,1024,4096]{2,1,0:T(8,128)(2,1)S(1)} %bitcast.478, ...), custom_call_target="tpu_custom_call", output_to_operand_aliasing={{0}: (7, {}), {1}: (8, {}), {2}: (9, {})} | custom-call | flops 31457280 | bytes 34603008 | tf_op jit(solution)/shard_map/pallas_call | solution.py:117
  1025.9 20.7 %shard_map.292 = (bf16[2,1024,4096]{2,1,0:T(8,128)(2,1)}, f32[2,1024,4096]{2,1,0:T(8,128)}, f32[2,1024,4096]{2,1,0:T(8,128)}) custom-call(s32[2]{0:T(128)S(1)} %pad_add_fusion.at, s32[5]{0:T(128)S(1)} %copy-done.21, bf16[2,1024,4096]{2,1,0:T(8,128)(2,1)S(1)} %bitcast.478, ...), custom_call_target="tpu_custom_call", output_to_operand_aliasing={{0}: (7, {}), {1}: (8, {}), {2}: (9, {})} | custom-call | flops 52428800 | bytes 57671680 | tf_op jit(solution)/shard_map/pallas_call | solution.py:117
  1046.6 13.2 %shard_map.293 = (bf16[2,1024,4096]{2,1,0:T(8,128)(2,1)}, f32[2,1024,4096]{2,1,0:T(8,128)}, f32[2,1024,4096]{2,1,0:T(8,128)}) custom-call(s32[2]{0:T(128)S(1)} %pad_add_fusion.at, s32[3]{0:T(128)S(1)} %copy-done.20, bf16[2,1024,4096]{2,1,0:T(8,128)(2,1)S(1)} %bitcast.478, ...), custom_call_target="tpu_custom_call", output_to_operand_aliasing={{0}: (7, {}), {1}: (8, {}), {2}: (9, {})} | custom-call | flops 31457280 | bytes 34603008 | tf_op jit(solution)/shard_map/pallas_call | solution.py:117
  1065.6 21.1 %shard_map.286 = (bf16[2,1024,4096]{2,1,0:T(8,128)(2,1)}, f32[2,1024,4096]{2,1,0:T(8,128)}, f32[2,1024,4096]{2,1,0:T(8,128)}) custom-call(s32[2]{0:T(128)S(1)} %pad_add_fusion.at, s32[5]{0:T(128)S(1)} %copy-done.21, bf16[2,1024,4096]{2,1,0:T(8,128)(2,1)S(1)} %copy-done, f32[2,1024,4096]{2,1,0:T(8,128)} %m.15, f32[2,1024,4096]{2,1,0:T(8,128)} %v.15, ...), custom_call_target="tpu_custom_call" | custom-call | flops 52428800 | bytes 57671680 | tf_op jit(solution)/shard_map/pallas_call | solution.py:117
  1086.7 13.2 %shard_map.287 = (bf16[2,1024,4096]{2,1,0:T(8,128)(2,1)}, f32[2,1024,4096]{2,1,0:T(8,128)}, f32[2,1024,4096]{2,1,0:T(8,128)}) custom-call(s32[2]{0:T(128)S(1)} %pad_add_fusion.at, s32[3]{0:T(128)S(1)} %copy-done.20, bf16[2,1024,4096]{2,1,0:T(8,128)(2,1)S(1)} %copy-done, ...), custom_call_target="tpu_custom_call", output_to_operand_aliasing={{0}: (7, {}), {1}: (8, {}), {2}: (9, {})} | custom-call | flops 31457280 | bytes 34603008 | tf_op jit(solution)/shard_map/pallas_call | solution.py:117
  1099.9 20.7 %shard_map.288 = (bf16[2,1024,4096]{2,1,0:T(8,128)(2,1)}, f32[2,1024,4096]{2,1,0:T(8,128)}, f32[2,1024,4096]{2,1,0:T(8,128)}) custom-call(s32[2]{0:T(128)S(1)} %pad_add_fusion.at, s32[5]{0:T(128)S(1)} %copy-done.21, bf16[2,1024,4096]{2,1,0:T(8,128)(2,1)S(1)} %copy-done, ...), custom_call_target="tpu_custom_call", output_to_operand_aliasing={{0}: (7, {}), {1}: (8, {}), {2}: (9, {})} | custom-call | flops 52428800 | bytes 57671680 | tf_op jit(solution)/shard_map/pallas_call | solution.py:117
  1120.7 13.6 %shard_map.289 = (bf16[2,1024,4096]{2,1,0:T(8,128)(2,1)}, f32[2,1024,4096]{2,1,0:T(8,128)}, f32[2,1024,4096]{2,1,0:T(8,128)}) custom-call(s32[2]{0:T(128)S(1)} %pad_add_fusion.at, s32[3]{0:T(128)S(1)} %copy-done.20, bf16[2,1024,4096]{2,1,0:T(8,128)(2,1)S(1)} %copy-done, ...), custom_call_target="tpu_custom_call", output_to_operand_aliasing={{0}: (7, {}), {1}: (8, {}), {2}: (9, {})} | custom-call | flops 31457280 | bytes 34603008 | tf_op jit(solution)/shard_map/pallas_call | solution.py:117
  1140.0 21.7 %shard_map.294 = (bf16[2,4096,1024]{2,1,0:T(8,128)(2,1)}, f32[2,4096,1024]{2,1,0:T(8,128)}, f32[2,4096,1024]{2,1,0:T(8,128)}) custom-call(s32[2]{0:T(128)S(1)} %pad_add_fusion.at, s32[5]{0:T(128)S(1)} %copy-done.21, bf16[2,4096,1024]{2,1,0:T(8,128)(2,1)S(1)} %copy-done.1, f32[2,4096,1024]{2,1,0:T(8,128)} %m.23, f32[2,4096,1024]{2,1,0:T(8,128)} %v.23, ...), custom_call_target="tpu_custom_call" | custom-call | flops 52428800 | bytes 57671680 | tf_op jit(solution)/shard_map/pallas_call | solution.py:117
  1161.8 13.6 %shard_map.295 = (bf16[2,4096,1024]{2,1,0:T(8,128)(2,1)}, f32[2,4096,1024]{2,1,0:T(8,128)}, f32[2,4096,1024]{2,1,0:T(8,128)}) custom-call(s32[2]{0:T(128)S(1)} %pad_add_fusion.at, s32[3]{0:T(128)S(1)} %copy-done.20, bf16[2,4096,1024]{2,1,0:T(8,128)(2,1)S(1)} %copy-done.1, ...), custom_call_target="tpu_custom_call", output_to_operand_aliasing={{0}: (7, {}), {1}: (8, {}), {2}: (9, {})} | custom-call | flops 31457280 | bytes 34603008 | tf_op jit(solution)/shard_map/pallas_call | solution.py:117
  1175.3 21.8 %shard_map.296 = (bf16[2,4096,1024]{2,1,0:T(8,128)(2,1)}, f32[2,4096,1024]{2,1,0:T(8,128)}, f32[2,4096,1024]{2,1,0:T(8,128)}) custom-call(s32[2]{0:T(128)S(1)} %pad_add_fusion.at, s32[5]{0:T(128)S(1)} %copy-done.21, bf16[2,4096,1024]{2,1,0:T(8,128)(2,1)S(1)} %copy-done.1, ...), custom_call_target="tpu_custom_call", output_to_operand_aliasing={{0}: (7, {}), {1}: (8, {}), {2}: (9, {})} | custom-call | flops 52428800 | bytes 57671680 | tf_op jit(solution)/shard_map/pallas_call | solution.py:117
  1197.1 13.6 %shard_map.297 = (bf16[2,4096,1024]{2,1,0:T(8,128)(2,1)}, f32[2,4096,1024]{2,1,0:T(8,128)}, f32[2,4096,1024]{2,1,0:T(8,128)}) custom-call(s32[2]{0:T(128)S(1)} %pad_add_fusion.at, s32[3]{0:T(128)S(1)} %copy-done.20, bf16[2,4096,1024]{2,1,0:T(8,128)(2,1)S(1)} %copy-done.1, ...), custom_call_target="tpu_custom_call", output_to_operand_aliasing={{0}: (7, {}), {1}: (8, {}), {2}: (9, {})} | custom-call | flops 31457280 | bytes 34603008 | tf_op jit(solution)/shard_map/pallas_call | solution.py:117
  (362 shorter events, 355.9 us)
Async XLA Ops:
  189.2 283.7 %collective-permute-start.85 = (bf16[8,256,1024]{2,1,0:T(8,128)(2,1)}, bf16[8,256,1024]{2,1,0:T(8,128)(2,1)}, u32[]{:S(2)}, u32[]{:S(2)}) collective-permute-start(bf16[8,256,1024]{2,1,0:T(8,128)(2,1)} %dynamic-slice_bitcast_fusion), channel_id=1, source_target_pairs={{0,1},{1,0},{2,3},{3,2},{4,5},{5,4},{6,7},{7,6},{8,9},{9,8},{10,11... | collective-permute-start | bytes 12582920 | tf_op jit(solution)/shard_map/ppermute | solution.py:47
  261.3 213.0 %collective-permute-start.17 = (bf16[8,64,4096]{2,1,0:T(8,128)(2,1)}, bf16[8,64,4096]{2,1,0:T(8,128)(2,1)}, u32[]{:S(2)}, u32[]{:S(2)}) collective-permute-start(bf16[8,64,4096]{2,1,0:T(8,128)(2,1)} %dynamic-slice_bitcast_fusion.4), channel_id=1, source_target_pairs={{0,1},{1,0},{2,3},{3,2},{4,5},{5,4},{6,7},{7,6},{8,9},{9,8},{10,11... | collective-permute-start | bytes 12582920 | tf_op jit(solution)/shard_map/ppermute | solution.py:47
  287.6 191.1 %collective-permute-start.51 = (bf16[8,64,4096]{2,1,0:T(8,128)(2,1)}, bf16[8,64,4096]{2,1,0:T(8,128)(2,1)}, u32[]{:S(2)}, u32[]{:S(2)}) collective-permute-start(bf16[8,64,4096]{2,1,0:T(8,128)(2,1)} %dynamic-slice_bitcast_fusion.2), channel_id=1, source_target_pairs={{0,1},{1,0},{2,3},{3,2},{4,5},{5,4},{6,7},{7,6},{8,9},{9,8},{10,11... | collective-permute-start | bytes 12582920 | tf_op jit(solution)/shard_map/ppermute | solution.py:47
  377.7 104.0 %collective-permute-start.68 = (bf16[8,256,1024]{2,1,0:T(8,128)(2,1)}, bf16[8,256,1024]{2,1,0:T(8,128)(2,1)}, u32[]{:S(2)}, u32[]{:S(2)}) collective-permute-start(bf16[8,256,1024]{2,1,0:T(8,128)(2,1)} %dynamic-slice_bitcast_fusion.1), channel_id=1, source_target_pairs={{0,1},{1,0},{2,3},{3,2},{4,5},{5,4},{6,7},{7,6},{8,9},{9,8},{10,11... | collective-permute-start | bytes 12582920 | tf_op jit(solution)/shard_map/ppermute | solution.py:47
  447.9 36.8 %collective-permute-start.34 = (bf16[8,64,4096]{2,1,0:T(8,128)(2,1)}, bf16[8,64,4096]{2,1,0:T(8,128)(2,1)}, u32[]{:S(2)}, u32[]{:S(2)}) collective-permute-start(bf16[8,64,4096]{2,1,0:T(8,128)(2,1)} %dynamic-slice_bitcast_fusion.3), channel_id=1, source_target_pairs={{0,1},{1,0},{2,3},{3,2},{4,5},{5,4},{6,7},{7,6},{8,9},{9,8},{10,11... | collective-permute-start | bytes 12582920 | tf_op jit(solution)/shard_map/ppermute | solution.py:47
  484.7 37.4 %collective-permute-start.69 = (bf16[256,1024]{1,0:T(8,128)(2,1)S(1)}, bf16[256,1024]{1,0:T(8,128)(2,1)S(1)}, u32[]{:S(2)}, u32[]{:S(2)}) collective-permute-start(bf16[256,1024]{1,0:T(8,128)(2,1)S(1)} %fusion.86), channel_id=1, source_target_pairs={{0,2},{2,4},{4,6},{6,14},{14,12},{12,10},{10,8},{8,0},{9,11},{11,1... | collective-permute-start | bytes 1572872 | tf_op jit(solution)/shard_map/ppermute | solution.py:47
  487.6 25.0 %collective-permute-start.35 = (bf16[64,4096]{1,0:T(8,128)(2,1)S(1)}, bf16[64,4096]{1,0:T(8,128)(2,1)S(1)}, u32[]{:S(2)}, u32[]{:S(2)}) collective-permute-start(bf16[64,4096]{1,0:T(8,128)(2,1)S(1)} %fusion.114), channel_id=1, source_target_pairs={{0,2},{2,4},{4,6},{6,14},{14,12},{12,10},{10,8},{8,0},{9,11},{11,1... | collective-permute-start | bytes 1572872 | tf_op jit(solution)/shard_map/ppermute | solution.py:47
  489.5 28.7 %collective-permute-start.1 = (bf16[64,4096]{1,0:T(8,128)(2,1)S(1)}, bf16[64,4096]{1,0:T(8,128)(2,1)S(1)}, u32[]{:S(2)}, u32[]{:S(2)}) collective-permute-start(bf16[64,4096]{1,0:T(8,128)(2,1)S(1)} %fusion.142), channel_id=1, source_target_pairs={{0,2},{2,4},{4,6},{6,14},{14,12},{12,10},{10,8},{8,0},{9,11},{11,1... | collective-permute-start | bytes 1572872 | tf_op jit(solution)/shard_map/ppermute | solution.py:47
  492.0 61.9 %collective-permute-start.87 = (bf16[256,1024]{1,0:T(8,128)(2,1)S(1)}, bf16[256,1024]{1,0:T(8,128)(2,1)S(1)}, u32[]{:S(2)}, u32[]{:S(2)}) collective-permute-start(bf16[256,1024]{1,0:T(8,128)(2,1)S(1)} %get-tuple-element.121), channel_id=1, source_target_pairs={{0,2},{2,4},{4,6},{6,14},{14,12},{12,10},{10,8},{8,0},{9,11},{11,1... | collective-permute-start | bytes 1572872 | tf_op jit(solution)/shard_map/ppermute | solution.py:47
  495.7 59.8 %collective-permute-start.90 = (bf16[256,1024]{1,0:T(8,128)(2,1)S(1)}, bf16[256,1024]{1,0:T(8,128)(2,1)S(1)}, u32[]{:S(2)}, u32[]{:S(2)}) collective-permute-start(bf16[256,1024]{1,0:T(8,128)(2,1)S(1)} %get-tuple-element.122), channel_id=1, source_target_pairs={{2,0},{4,2},{6,4},{14,6},{12,14},{10,12},{8,10},{0,8},{11,9},{13,1... | collective-permute-start | bytes 1572872 | tf_op jit(solution)/shard_map/ppermute | solution.py:47
  537.1 54.1 %collective-permute-start.70 = (bf16[256,1024]{1,0:T(8,128)(2,1)S(1)}, bf16[256,1024]{1,0:T(8,128)(2,1)S(1)}, u32[]{:S(2)}, u32[]{:S(2)}) collective-permute-start(bf16[256,1024]{1,0:T(8,128)(2,1)S(1)} %get-tuple-element.127), channel_id=1, source_target_pairs={{0,2},{2,4},{4,6},{6,14},{14,12},{12,10},{10,8},{8,0},{9,11},{11,1... | collective-permute-start | bytes 1572872 | tf_op jit(solution)/shard_map/ppermute | solution.py:47
  553.9 38.9 %collective-permute-start.73 = (bf16[256,1024]{1,0:T(8,128)(2,1)S(1)}, bf16[256,1024]{1,0:T(8,128)(2,1)S(1)}, u32[]{:S(2)}, u32[]{:S(2)}) collective-permute-start(bf16[256,1024]{1,0:T(8,128)(2,1)S(1)} %get-tuple-element.128), channel_id=1, source_target_pairs={{2,0},{4,2},{6,4},{14,6},{12,14},{10,12},{8,10},{0,8},{11,9},{13,1... | collective-permute-start | bytes 1572872 | tf_op jit(solution)/shard_map/ppermute | solution.py:47
  566.3 62.0 %collective-permute-start.88 = (bf16[256,1024]{1,0:T(8,128)(2,1)S(1)}, bf16[256,1024]{1,0:T(8,128)(2,1)S(1)}, u32[]{:S(2)}, u32[]{:S(2)}) collective-permute-start(bf16[256,1024]{1,0:T(8,128)(2,1)S(1)} %get-tuple-element.119), channel_id=1, source_target_pairs={{0,2},{2,4},{4,6},{6,14},{14,12},{12,10},{10,8},{8,0},{9,11},{11,1... | collective-permute-start | bytes 1572872 | tf_op jit(solution)/shard_map/ppermute | solution.py:47
  591.2 38.5 %collective-permute-start.91 = (bf16[256,1024]{1,0:T(8,128)(2,1)S(1)}, bf16[256,1024]{1,0:T(8,128)(2,1)S(1)}, u32[]{:S(2)}, u32[]{:S(2)}) collective-permute-start(bf16[256,1024]{1,0:T(8,128)(2,1)S(1)} %get-tuple-element.120), channel_id=1, source_target_pairs={{2,0},{4,2},{6,4},{14,6},{12,14},{10,12},{8,10},{0,8},{11,9},{13,1... | collective-permute-start | bytes 1572872 | tf_op jit(solution)/shard_map/ppermute | solution.py:47
  595.4 28.4 %collective-permute-start.57 = (bf16[64,4096]{1,0:T(8,128)(2,1)S(1)}, bf16[64,4096]{1,0:T(8,128)(2,1)S(1)}, u32[]{:S(2)}, u32[]{:S(2)}) collective-permute-start(bf16[64,4096]{1,0:T(8,128)(2,1)S(1)} %get-tuple-element.132), channel_id=1, source_target_pairs={{2,0},{4,2},{6,4},{14,6},{12,14},{10,12},{8,10},{0,8},{11,9},{13,1... | collective-permute-start | bytes 1572872 | tf_op jit(solution)/shard_map/ppermute | solution.py:47
  601.3 64.2 %collective-permute-start.71 = (bf16[256,1024]{1,0:T(8,128)(2,1)S(1)}, bf16[256,1024]{1,0:T(8,128)(2,1)S(1)}, u32[]{:S(2)}, u32[]{:S(2)}) collective-permute-start(bf16[256,1024]{1,0:T(8,128)(2,1)S(1)} %get-tuple-element.125), channel_id=1, source_target_pairs={{0,2},{2,4},{4,6},{6,14},{14,12},{12,10},{10,8},{8,0},{9,11},{11,1... | collective-permute-start | bytes 1572872 | tf_op jit(solution)/shard_map/ppermute | solution.py:47
  607.6 25.0 %collective-permute-start.37 = (bf16[64,4096]{1,0:T(8,128)(2,1)S(1)}, bf16[64,4096]{1,0:T(8,128)(2,1)S(1)}, u32[]{:S(2)}, u32[]{:S(2)}) collective-permute-start(bf16[64,4096]{1,0:T(8,128)(2,1)S(1)} %get-tuple-element.137), channel_id=1, source_target_pairs={{0,2},{2,4},{4,6},{6,14},{14,12},{12,10},{10,8},{8,0},{9,11},{11,1... | collective-permute-start | bytes 1572872 | tf_op jit(solution)/shard_map/ppermute | solution.py:47
  628.3 38.6 %collective-permute-start.74 = (bf16[256,1024]{1,0:T(8,128)(2,1)S(1)}, bf16[256,1024]{1,0:T(8,128)(2,1)S(1)}, u32[]{:S(2)}, u32[]{:S(2)}) collective-permute-start(bf16[256,1024]{1,0:T(8,128)(2,1)S(1)} %get-tuple-element.126), channel_id=1, source_target_pairs={{2,0},{4,2},{6,4},{14,6},{12,14},{10,12},{8,10},{0,8},{11,9},{13,1... | collective-permute-start | bytes 1572872 | tf_op jit(solution)/shard_map/ppermute | solution.py:47
  632.6 28.5 %collective-permute-start.6 = (bf16[64,4096]{1,0:T(8,128)(2,1)S(1)}, bf16[64,4096]{1,0:T(8,128)(2,1)S(1)}, u32[]{:S(2)}, u32[]{:S(2)}) collective-permute-start(bf16[64,4096]{1,0:T(8,128)(2,1)S(1)} %get-tuple-element.150), channel_id=1, source_target_pairs={{2,0},{4,2},{6,4},{14,6},{12,14},{10,12},{8,10},{0,8},{11,9},{13,1... | collective-permute-start | bytes 1572872 | tf_op jit(solution)/shard_map/ppermute | solution.py:47
  638.6 63.7 %collective-permute-start.89 = (bf16[256,1024]{1,0:T(8,128)(2,1)S(1)}, bf16[256,1024]{1,0:T(8,128)(2,1)S(1)}, u32[]{:S(2)}, u32[]{:S(2)}) collective-permute-start(bf16[256,1024]{1,0:T(8,128)(2,1)S(1)} %get-tuple-element.117), channel_id=1, source_target_pairs={{0,2},{2,4},{4,6},{6,14},{14,12},{12,10},{10,8},{8,0},{9,11},{11,1... | collective-permute-start | bytes 1572872 | tf_op jit(solution)/shard_map/ppermute | solution.py:47
  644.5 25.4 %collective-permute-start.21 = (bf16[64,4096]{1,0:T(8,128)(2,1)S(1)}, bf16[64,4096]{1,0:T(8,128)(2,1)S(1)}, u32[]{:S(2)}, u32[]{:S(2)}) collective-permute-start(bf16[64,4096]{1,0:T(8,128)(2,1)S(1)} %get-tuple-element.141), channel_id=1, source_target_pairs={{0,2},{2,4},{4,6},{6,14},{14,12},{12,10},{10,8},{8,0},{9,11},{11,1... | collective-permute-start | bytes 1572872 | tf_op jit(solution)/shard_map/ppermute | solution.py:47
  665.6 37.0 %collective-permute-start.92 = (bf16[256,1024]{1,0:T(8,128)(2,1)S(1)}, bf16[256,1024]{1,0:T(8,128)(2,1)S(1)}, u32[]{:S(2)}, u32[]{:S(2)}) collective-permute-start(bf16[256,1024]{1,0:T(8,128)(2,1)S(1)} %get-tuple-element.118), channel_id=1, source_target_pairs={{2,0},{4,2},{6,4},{14,6},{12,14},{10,12},{8,10},{0,8},{11,9},{13,1... | collective-permute-start | bytes 1572872 | tf_op jit(solution)/shard_map/ppermute | solution.py:47
  669.8 28.5 %collective-permute-start.58 = (bf16[64,4096]{1,0:T(8,128)(2,1)S(1)}, bf16[64,4096]{1,0:T(8,128)(2,1)S(1)}, u32[]{:S(2)}, u32[]{:S(2)}) collective-permute-start(bf16[64,4096]{1,0:T(8,128)(2,1)S(1)} %get-tuple-element.130), channel_id=1, source_target_pairs={{2,0},{4,2},{6,4},{14,6},{12,14},{10,12},{8,10},{0,8},{11,9},{13,1... | collective-permute-start | bytes 1572872 | tf_op jit(solution)/shard_map/ppermute | solution.py:47
  675.9 57.3 %collective-permute-start.72 = (bf16[256,1024]{1,0:T(8,128)(2,1)S(1)}, bf16[256,1024]{1,0:T(8,128)(2,1)S(1)}, u32[]{:S(2)}, u32[]{:S(2)}) collective-permute-start(bf16[256,1024]{1,0:T(8,128)(2,1)S(1)} %get-tuple-element.123), channel_id=1, source_target_pairs={{0,2},{2,4},{4,6},{6,14},{14,12},{12,10},{10,8},{8,0},{9,11},{11,1... | collective-permute-start | bytes 1572872 | tf_op jit(solution)/shard_map/ppermute | solution.py:47
  681.1 25.8 %collective-permute-start.38 = (bf16[64,4096]{1,0:T(8,128)(2,1)S(1)}, bf16[64,4096]{1,0:T(8,128)(2,1)S(1)}, u32[]{:S(2)}, u32[]{:S(2)}) collective-permute-start(bf16[64,4096]{1,0:T(8,128)(2,1)S(1)} %get-tuple-element.135), channel_id=1, source_target_pairs={{0,2},{2,4},{4,6},{6,14},{14,12},{12,10},{10,8},{8,0},{9,11},{11,1... | collective-permute-start | bytes 1572872 | tf_op jit(solution)/shard_map/ppermute | solution.py:47
  702.3 32.7 %collective-permute-start.75 = (bf16[256,1024]{1,0:T(8,128)(2,1)S(1)}, bf16[256,1024]{1,0:T(8,128)(2,1)S(1)}, u32[]{:S(2)}, u32[]{:S(2)}) collective-permute-start(bf16[256,1024]{1,0:T(8,128)(2,1)S(1)} %get-tuple-element.124), channel_id=1, source_target_pairs={{2,0},{4,2},{6,4},{14,6},{12,14},{10,12},{8,10},{0,8},{11,9},{13,1... | collective-permute-start | bytes 1572872 | tf_op jit(solution)/shard_map/ppermute | solution.py:47
  712.6 92.0 %collective-permute-start.96 = (bf16[256,1024]{1,0:T(8,128)(2,1)S(1)}, bf16[256,1024]{1,0:T(8,128)(2,1)S(1)}, u32[]{:S(2)}, u32[]{:S(2)}) collective-permute-start(bf16[256,1024]{1,0:T(8,128)(2,1)S(1)} %get-tuple-element.102), channel_id=1, source_target_pairs={{2,0},{4,2},{6,4},{14,6},{12,14},{10,12},{8,10},{0,8},{11,9},{13,1... | collective-permute-start | bytes 1572872 | tf_op jit(solution)/shard_map/ppermute | solution.py:47
  717.6 87.1 %collective-permute-start.93 = (bf16[256,1024]{1,0:T(8,128)(2,1)S(1)}, bf16[256,1024]{1,0:T(8,128)(2,1)S(1)}, u32[]{:S(2)}, u32[]{:S(2)}) collective-permute-start(bf16[256,1024]{1,0:T(8,128)(2,1)S(1)} %get-tuple-element.102), channel_id=1, source_target_pairs={{0,2},{2,4},{4,6},{6,14},{14,12},{12,10},{10,8},{8,0},{9,11},{11,1... | collective-permute-start | bytes 1572872 | tf_op jit(solution)/shard_map/ppermute | solution.py:47
  735.0 27.0 %collective-permute-start.62 = (bf16[64,4096]{1,0:T(8,128)(2,1)S(1)}, bf16[64,4096]{1,0:T(8,128)(2,1)S(1)}, u32[]{:S(2)}, u32[]{:S(2)}) collective-permute-start(bf16[64,4096]{1,0:T(8,128)(2,1)S(1)} %get-tuple-element.106), channel_id=1, source_target_pairs={{2,0},{4,2},{6,4},{14,6},{12,14},{10,12},{8,10},{0,8},{11,9},{13,1... | collective-permute-start | bytes 1572872 | tf_op jit(solution)/shard_map/ppermute | solution.py:47
  750.8 82.3 %collective-permute-start.79 = (bf16[256,1024]{1,0:T(8,128)(2,1)S(1)}, bf16[256,1024]{1,0:T(8,128)(2,1)S(1)}, u32[]{:S(2)}, u32[]{:S(2)}) collective-permute-start(bf16[256,1024]{1,0:T(8,128)(2,1)S(1)} %get-tuple-element.104), channel_id=1, source_target_pairs={{2,0},{4,2},{6,4},{14,6},{12,14},{10,12},{8,10},{0,8},{11,9},{13,1... | collective-permute-start | bytes 1572872 | tf_op jit(solution)/shard_map/ppermute | solution.py:47
  755.4 62.7 %collective-permute-start.76 = (bf16[256,1024]{1,0:T(8,128)(2,1)S(1)}, bf16[256,1024]{1,0:T(8,128)(2,1)S(1)}, u32[]{:S(2)}, u32[]{:S(2)}) collective-permute-start(bf16[256,1024]{1,0:T(8,128)(2,1)S(1)} %get-tuple-element.104), channel_id=1, source_target_pairs={{0,2},{2,4},{4,6},{6,14},{14,12},{12,10},{10,8},{8,0},{9,11},{11,1... | collective-permute-start | bytes 1572872 | tf_op jit(solution)/shard_map/ppermute | solution.py:47
  804.7 28.5 %collective-permute-start.97 = (bf16[256,1024]{1,0:T(8,128)(2,1)S(1)}, bf16[256,1024]{1,0:T(8,128)(2,1)S(1)}, u32[]{:S(2)}, u32[]{:S(2)}) collective-permute-start(bf16[256,1024]{1,0:T(8,128)(2,1)S(1)} %collective-permute-done.96), channel_id=1, source_target_pairs={{2,0},{4,2},{6,4},{14,6},{12,14},{10,12},{8,10},{0,8},{11,9},{13,1... | collective-permute-start | bytes 1572872 | tf_op jit(solution)/shard_map/ppermute | solution.py:47
  833.1 39.3 %collective-permute-start.77 = (bf16[256,1024]{1,0:T(8,128)(2,1)S(1)}, bf16[256,1024]{1,0:T(8,128)(2,1)S(1)}, u32[]{:S(2)}, u32[]{:S(2)}) collective-permute-start(bf16[256,1024]{1,0:T(8,128)(2,1)S(1)} %collective-permute-done.76), channel_id=1, source_target_pairs={{0,2},{2,4},{4,6},{6,14},{14,12},{12,10},{10,8},{8,0},{9,11},{11,1... | collective-permute-start | bytes 1572872 | tf_op jit(solution)/shard_map/ppermute | solution.py:47
  833.2 41.3 %collective-permute-start.46 = (bf16[64,4096]{1,0:T(8,128)(2,1)S(1)}, bf16[64,4096]{1,0:T(8,128)(2,1)S(1)}, u32[]{:S(2)}, u32[]{:S(2)}) collective-permute-start(bf16[64,4096]{1,0:T(8,128)(2,1)S(1)} %collective-permute-done.45), channel_id=1, source_target_pairs={{2,0},{4,2},{6,4},{14,6},{12,14},{10,12},{8,10},{0,8},{11,9},{13,1... | collective-permute-start | bytes 1572872 | tf_op jit(solution)/shard_map/ppermute | solution.py:47
  835.2 39.2 %collective-permute-start.43 = (bf16[64,4096]{1,0:T(8,128)(2,1)S(1)}, bf16[64,4096]{1,0:T(8,128)(2,1)S(1)}, u32[]{:S(2)}, u32[]{:S(2)}) collective-permute-start(bf16[64,4096]{1,0:T(8,128)(2,1)S(1)} %collective-permute-done.42), channel_id=1, source_target_pairs={{0,2},{2,4},{4,6},{6,14},{14,12},{12,10},{10,8},{8,0},{9,11},{11,1... | collective-permute-start | bytes 1572872 | tf_op jit(solution)/shard_map/ppermute | solution.py:47
  844.3 32.3 %collective-permute-start.12 = (bf16[64,4096]{1,0:T(8,128)(2,1)S(1)}, bf16[64,4096]{1,0:T(8,128)(2,1)S(1)}, u32[]{:S(2)}, u32[]{:S(2)}) collective-permute-start(bf16[64,4096]{1,0:T(8,128)(2,1)S(1)} %collective-permute-done.11), channel_id=1, source_target_pairs={{2,0},{4,2},{6,4},{14,6},{12,14},{10,12},{8,10},{0,8},{11,9},{13,1... | collective-permute-start | bytes 1572872 | tf_op jit(solution)/shard_map/ppermute | solution.py:47
  872.4 31.8 %collective-permute-start.30 = (bf16[64,4096]{1,0:T(8,128)(2,1)S(1)}, bf16[64,4096]{1,0:T(8,128)(2,1)S(1)}, u32[]{:S(2)}, u32[]{:S(2)}) collective-permute-start(bf16[64,4096]{1,0:T(8,128)(2,1)S(1)} %collective-permute-done.29), channel_id=1, source_target_pairs={{2,0},{4,2},{6,4},{14,6},{12,14},{10,12},{8,10},{0,8},{11,9},{13,1... | collective-permute-start | bytes 1572872 | tf_op jit(solution)/shard_map/ppermute | solution.py:47
  874.4 29.7 %collective-permute-start.27 = (bf16[64,4096]{1,0:T(8,128)(2,1)S(1)}, bf16[64,4096]{1,0:T(8,128)(2,1)S(1)}, u32[]{:S(2)}, u32[]{:S(2)}) collective-permute-start(bf16[64,4096]{1,0:T(8,128)(2,1)S(1)} %collective-permute-done.26), channel_id=1, source_target_pairs={{0,2},{2,4},{4,6},{6,14},{14,12},{12,10},{10,8},{8,0},{9,11},{11,1... | collective-permute-start | bytes 1572872 | tf_op jit(solution)/shard_map/ppermute | solution.py:47
  876.5 25.3 %collective-permute-start.95 = (bf16[256,1024]{1,0:T(8,128)(2,1)S(1)}, bf16[256,1024]{1,0:T(8,128)(2,1)S(1)}, u32[]{:S(2)}, u32[]{:S(2)}) collective-permute-start(bf16[256,1024]{1,0:T(8,128)(2,1)S(1)} %collective-permute-done.94), channel_id=1, source_target_pairs={{0,2},{2,4},{4,6},{6,14},{14,12},{12,10},{10,8},{8,0},{9,11},{11,1... | collective-permute-start | bytes 1572872 | tf_op jit(solution)/shard_map/ppermute | solution.py:47
  904.2 27.8 %collective-permute-start.31 = (bf16[64,4096]{1,0:T(8,128)(2,1)S(1)}, bf16[64,4096]{1,0:T(8,128)(2,1)S(1)}, u32[]{:S(2)}, u32[]{:S(2)}) collective-permute-start(bf16[64,4096]{1,0:T(8,128)(2,1)S(1)} %collective-permute-done.27), channel_id=1, source_target_pairs={{0,2},{2,4},{4,6},{6,14},{14,12},{12,10},{10,8},{8,0},{9,11},{11,1... | collective-permute-start | bytes 1572872 | tf_op jit(solution)/shard_map/ppermute | solution.py:47
  909.7 28.0 %collective-permute-start.44 = (bf16[64,4096]{1,0:T(8,128)(2,1)S(1)}, bf16[64,4096]{1,0:T(8,128)(2,1)S(1)}, u32[]{:S(2)}, u32[]{:S(2)}) collective-permute-start(bf16[64,4096]{1,0:T(8,128)(2,1)S(1)} %collective-permute-done.43), channel_id=1, source_target_pairs={{0,2},{2,4},{4,6},{6,14},{14,12},{12,10},{10,8},{8,0},{9,11},{11,1... | collective-permute-start | bytes 1572872 | tf_op jit(solution)/shard_map/ppermute | solution.py:47
  932.3 45.4 %collective-permute-start.33 = (bf16[5,64,4096]{2,1,0:T(8,128)(2,1)S(1)}, bf16[5,64,4096]{2,1,0:T(8,128)(2,1)S(1)}, u32[]{:S(2)}, u32[]{:S(2)}) collective-permute-start(bf16[5,64,4096]{2,1,0:T(8,128)(2,1)S(1)} %bitcast_dynamic-update-slice_fusion.20.mine), channel_id=1, source_target_pairs={{0,1},{1,0},{2,3},{3,2},{4,5},{5,4},{6,7},{7,6},{8,9},{9,8},{10,11... | collective-permute-start | bytes 7864328 | tf_op jit(solution)/shard_map/ppermute | solution.py:47
  954.5 26.8 %collective-permute-start.67 = (bf16[5,64,4096]{2,1,0:T(8,128)(2,1)S(1)}, bf16[5,64,4096]{2,1,0:T(8,128)(2,1)S(1)}, u32[]{:S(2)}, u32[]{:S(2)}) collective-permute-start(bf16[5,64,4096]{2,1,0:T(8,128)(2,1)S(1)} %bitcast_dynamic-update-slice_fusion.10.mine), channel_id=1, source_target_pairs={{0,1},{1,0},{2,3},{3,2},{4,5},{5,4},{6,7},{7,6},{8,9},{9,8},{10,11... | collective-permute-start | bytes 7864328 | tf_op jit(solution)/shard_map/ppermute | solution.py:47
  980.0 154.2 %collective-permute-start.101 = (bf16[5,256,1024]{2,1,0:T(8,128)(2,1)}, bf16[5,256,1024]{2,1,0:T(8,128)(2,1)}, u32[]{:S(2)}, u32[]{:S(2)}) collective-permute-start(bf16[5,256,1024]{2,1,0:T(8,128)(2,1)} %bitcast_dynamic-update-slice_fusion.mine), channel_id=1, source_target_pairs={{0,1},{1,0},{2,3},{3,2},{4,5},{5,4},{6,7},{7,6},{8,9},{9,8},{10,11... | collective-permute-start | bytes 7864328 | tf_op jit(solution)/shard_map/ppermute | solution.py:47
  981.3 194.0 %collective-permute-start.84 = (bf16[5,256,1024]{2,1,0:T(8,128)(2,1)}, bf16[5,256,1024]{2,1,0:T(8,128)(2,1)}, u32[]{:S(2)}, u32[]{:S(2)}) collective-permute-start(bf16[5,256,1024]{2,1,0:T(8,128)(2,1)} %bitcast_dynamic-update-slice_fusion.5.mine), channel_id=1, source_target_pairs={{0,1},{1,0},{2,3},{3,2},{4,5},{5,4},{6,7},{7,6},{8,9},{9,8},{10,11... | collective-permute-start | bytes 7864328 | tf_op jit(solution)/shard_map/ppermute | solution.py:47
  987.8 173.9 %collective-permute-start.100 = (bf16[3,256,1024]{2,1,0:T(8,128)(2,1)}, bf16[3,256,1024]{2,1,0:T(8,128)(2,1)}, u32[]{:S(2)}, u32[]{:S(2)}) collective-permute-start(bf16[3,256,1024]{2,1,0:T(8,128)(2,1)} %pad_maximum_fusion.5.mine), channel_id=1, source_target_pairs={{0,1},{1,0},{2,3},{3,2},{4,5},{5,4},{6,7},{7,6},{8,9},{9,8},{10,11... | collective-permute-start | bytes 4718600 | tf_op jit(solution)/shard_map/ppermute | solution.py:47
  988.0 132.6 %collective-permute-start.15 = (bf16[3,64,4096]{2,1,0:T(8,128)(2,1)}, bf16[3,64,4096]{2,1,0:T(8,128)(2,1)}, u32[]{:S(2)}, u32[]{:S(2)}) collective-permute-start(bf16[3,64,4096]{2,1,0:T(8,128)(2,1)} %pad_maximum_fusion.mine), channel_id=1, source_target_pairs={{0,1},{1,0},{2,3},{3,2},{4,5},{5,4},{6,7},{7,6},{8,9},{9,8},{10,11... | collective-permute-start | bytes 4718600 | tf_op jit(solution)/shard_map/ppermute | solution.py:47
  991.5 205.6 %collective-permute-start.83 = (bf16[3,256,1024]{2,1,0:T(8,128)(2,1)}, bf16[3,256,1024]{2,1,0:T(8,128)(2,1)}, u32[]{:S(2)}, u32[]{:S(2)}) collective-permute-start(bf16[3,256,1024]{2,1,0:T(8,128)(2,1)} %pad_maximum_fusion.4.mine), channel_id=1, source_target_pairs={{0,1},{1,0},{2,3},{3,2},{4,5},{5,4},{6,7},{7,6},{8,9},{9,8},{10,11... | collective-permute-start | bytes 4718600 | tf_op jit(solution)/shard_map/ppermute | solution.py:47
  (105 other events, 2027.0 us)
